TPU v7x, 16 devices: a 4x2x1 block of a 4x4x8 slice. The times are simulated.
16 devices in a mesh: rep: 2 (over y, z), dp: 8 (over x, core).
Axes of the slice: x: 4, y: 2, z: 1, core: 2. Of those that a mesh axis runs over, the one named last changes fastest.
The devices are a block of a 4x4x8 slice.
Arguments:
- x: bfloat16 [16, 2048, 768], P(('rep', 'dp')), parts along dimension 0
- dy: bfloat16 [16, 2048, 768], P(('rep', 'dp')), parts along dimension 0
- w_gate: bfloat16 [2, 768, 3072], P(None, 'dp')
- w_up: bfloat16 [2, 768, 3072], P(None, 'dp')
- w_down: bfloat16 [2, 3072, 768], P(None, 'dp')
Outputs:
- output 1: bfloat16 [16, 2048, 768], P(('rep', 'dp')), parts along dimension 0
- output 2: bfloat16 [4, 768, 3072], P('rep', 'dp'), parts along dimension 0
- output 3: bfloat16 [4, 768, 3072], P('rep', 'dp'), parts along dimension 0
- output 4: bfloat16 [4, 3072, 768], P('rep', 'dp'), parts along dimension 0
There are 2 independent parts. A program takes and returns all parts, laid end to end along the dimension named above; an argument that names none is the same for every part.
All inputs are finite; a program needn't handle non-finite values.
Results may differ from a plain program's by a relative error of at most 0.018.
Values are sent between devices in bfloat16 or wider.
A program may use at most 768 MiB of HBM per device.

v0:
```python
import jax
import jax.numpy as jnp
from jax import lax

NAMES = ("w_gate", "w_up", "w_down")


def matmul(a, w):
    return jnp.dot(a, w, preferred_element_type=jnp.float32).astype(jnp.bfloat16)


def normed(h):
    wide = h.astype(jnp.float32)
    scale = lax.rsqrt(jnp.mean(wide**2, -1, keepdims=True) + 1e-6)
    return (wide * scale).astype(jnp.bfloat16)


def layer(h, w):
    a = normed(h)
    gate = jnp.dot(a, w["w_gate"], preferred_element_type=jnp.float32)
    up = jnp.dot(a, w["w_up"], preferred_element_type=jnp.float32)
    return h + matmul((jax.nn.silu(gate) * up).astype(jnp.bfloat16), w["w_down"])


def stack(weights, h):
    for number in range(weights["w_gate"].shape[0]):
        h = layer(h, {name: w[number] for name, w in weights.items()})
    return h


def solution(mesh):
    groups = mesh.shape["rep"]

    def step(x, dy, *weights):
        shape = x.shape
        x, dy = (t.reshape(groups, -1, *t.shape[1:]) for t in (x, dy))

        def of_a_group(x, dy):
            _, back = jax.vjp(stack, dict(zip(NAMES, weights, strict=True)), x)
            by_weights, by_x = back(dy)
            return (by_x, *(by_weights[name] for name in NAMES))

        by_x, *by_weights = jax.vmap(of_a_group)(x, dy)
        return (by_x.reshape(shape), *(t.reshape(-1, *t.shape[2:]) for t in by_weights))

    return step
```

profile of v0, /device:TPU:112, one launch (start us, length us, event | category | flops | bytes accessed | tf_op | source)
XLA Modules:
  0.0 634.5 jit_solution(15397887409925574773)
XLA Ops:
  25.6 17.1 %all-gather.30.cloned.1.call-done = bf16[1,768,3072]{2,1,0:T(8,128)(2,1)} async-done(((bf16[1,96,3072]{2,1,0:T(8,128)(2,1)}), bf16[1,768,3072]{2,1,0:T(8,128)(2,1)}) %all-gather.30.cloned.1.call-update) | async-done | bytes 4718608 | tf_op jit(solution)/vmap(jvp())/squeeze | solution.py:27
  42.7 15.9 %fusion.68 = f32[2048,3072]{1,0:T(8,128)} fusion(bf16[1,768,3072]{2,1,0:T(8,128)(2,1)} %all-gather.30.cloned.1.call-done, bf16[1,2048,768]{2,1,0:T(8,128)(2,1)S(1)} %copy-done.4, f32[2048]{0:T(1024)S(1)} %get-tuple-element.13), kind=kOutput, calls=%fused_computation.87 | convolution fusion | flops 9668395008 | bytes 33038336 | tf_op jit(solution)/vmap(jvp())/dot_general | solution.py:20
  58.6 16.2 %all-gather.32.cloned.1.call-done = bf16[1,768,3072]{2,1,0:T(8,128)(2,1)} async-done(((bf16[1,96,3072]{2,1,0:T(8,128)(2,1)}), bf16[1,768,3072]{2,1,0:T(8,128)(2,1)}) %all-gather.32.cloned.1.call-update) | async-done | bytes 4718608 | tf_op jit(solution)/vmap(jvp())/squeeze | solution.py:27
  74.8 15.9 %fusion.64 = f32[2048,3072]{1,0:T(8,128)} fusion(bf16[1,768,3072]{2,1,0:T(8,128)(2,1)} %all-gather.32.cloned.1.call-done, bf16[1,2048,768]{2,1,0:T(8,128)(2,1)S(1)} %copy-done.4, f32[2048]{0:T(1024)S(1)} %get-tuple-element.13), kind=kOutput, calls=%fused_computation.83 | convolution fusion | flops 9668395008 | bytes 33038336 | tf_op jit(solution)/vmap(jvp())/dot_general | solution.py:21
  90.6 21.9 %fusion.24 = bf16[2048,3072]{1,0:T(8,128)(2,1)} fusion(f32[2048,3072]{1,0:T(8,128)} %fusion.64, f32[2048,3072]{1,0:T(8,128)} %fusion.68), kind=kLoop, calls=%fused_computation.34 | loop fusion | flops 37748736 | bytes 62914560
  112.6 16.1 %fusion.40 = (f32[2048]{0:T(1024)S(1)}, bf16[1,1,2048,768]{2,3,1,0:T(8,128)(2,1)}) fusion(bf16[2048,3072]{1,0:T(8,128)(2,1)} %fusion.24, bf16[1,3072,768]{2,1,0:T(8,128)(2,1)} %all-gather.34.cloned.1.call-done, bf16[1,2048,768]{1,2,0:T(8,128)(2,1)S(1)} %copy-done.5), kind=kOutput, calls=%fused_computation.62 | convolution fusion | flops 9671538688 | bytes 23601152 | tf_op jit(solution)/vmap(jvp())/dot_general | solution.py:9
  138.2 17.9 %fusion.58 = f32[2048,3072]{1,0:T(8,128)} fusion(bf16[1,768,3072]{2,1,0:T(8,128)(2,1)} %all-gather.36.cloned.1.call-done, bf16[1,1,2048,768]{2,3,1,0:T(8,128)(2,1)} %get-tuple-element.15, f32[2048]{0:T(1024)S(1)} %bitcast.305), kind=kOutput, calls=%fused_computation.77 | convolution fusion | flops 9668395008 | bytes 33038336 | tf_op jit(solution)/vmap(jvp())/dot_general | solution.py:20
  156.1 14.1 %all-gather.40.cloned.1.call-done = bf16[1,768,3072]{2,1,0:T(8,128)(2,1)} async-done(((bf16[1,96,3072]{2,1,0:T(8,128)(2,1)}), bf16[1,768,3072]{2,1,0:T(8,128)(2,1)}) %all-gather.40.cloned.1.call-update) | async-done | bytes 4718608 | tf_op jit(solution)/vmap(jvp())/squeeze | solution.py:27
  170.2 15.8 %fusion.52 = f32[2048,3072]{1,0:T(8,128)} fusion(bf16[1,768,3072]{2,1,0:T(8,128)(2,1)} %all-gather.40.cloned.1.call-done, bf16[1,1,2048,768]{2,3,1,0:T(8,128)(2,1)S(1)} %copy-done.10, f32[2048]{0:T(1024)S(1)} %bitcast.306), kind=kOutput, calls=%fused_computation.71 | convolution fusion | flops 9668395008 | bytes 33038336 | tf_op jit(solution)/vmap(jvp())/dot_general | solution.py:21
  186.0 15.6 %all-gather.38.cloned.1.call-done = bf16[1,3072,768]{2,1,0:T(8,128)(2,1)} async-done(((bf16[1,384,768]{2,1,0:T(8,128)(2,1)}), bf16[1,3072,768]{2,1,0:T(8,128)(2,1)}) %all-gather.38.cloned.1.call-update) | async-done | bytes 4718608 | tf_op jit(solution)/vmap(jvp())/squeeze | solution.py:27
  214.6 22.9 %fusion.4 = bf16[2048,3072]{1,0:T(8,128)(2,1)S(1)} fusion(f32[2048,3072]{1,0:T(8,128)} %fusion.58, f32[2048,3072]{1,0:T(8,128)} %fusion.52, bf16[2048,3072]{1,0:T(8,128)(2,1)S(1)} %convolution_convert_fusion.1), kind=kLoop, calls=%fused_computation.10 | loop fusion | flops 75497472 | bytes 75497472
  254.7 18.0 %fusion.42 = (f32[2048]{0:T(1024)S(1)}, bf16[2048,768]{0,1:T(8,128)(2,1)}) fusion(bf16[1,1,2048,768]{2,3,1,0:T(8,128)(2,1)} %get-tuple-element.15, bf16[2048,768]{0,1:T(8,128)(2,1)} %fusion.76, bf16[1,768,3072]{2,1,0:T(8,128)(2,1)} %all-gather.40.cloned.1.call-done, bf16[2048,3072]{1,0:T(8,128)(2,1)S(1)} %convolution_convert_fusion.1, f32[2048,3072]{1,0:T(8,128)} %fusion.58), kind=kOutput, calls=%fused_computation.64 | convolution fusion | flops 9710860288 | bytes 51912704 | tf_op jit(solution)/vmap(transpose(jvp()))/dot_general | solution.py:21
  278.6 15.8 %convolution_bitcast_fusion = f32[1,3072,768]{2,1,0:T(8,128)} fusion(bf16[2048,3072]{1,0:T(8,128)(2,1)} %fusion.24, bf16[1,1,2048,768]{2,3,1,0:T(8,128)(2,1)S(1)} %fusion.93), kind=kOutput, calls=%fused_computation.65 | convolution fusion | flops 9663676416 | bytes 25165824 | tf_op jit(solution)/vmap(transpose(jvp()))/dot_general | solution.py:9
  296.2 23.8 %fusion.43 = f32[1,3072,768]{2,1,0:T(8,128)} fusion(f32[2048,3072]{1,0:T(8,128)} %fusion.52, f32[2048,3072]{1,0:T(8,128)} %fusion.58, bf16[1,2048,768]{2,1,0:T(8,128)(2,1)S(1)} %copy-done.9), kind=kOutput, calls=%fused_computation.68 | convolution fusion | flops 9701425152 | bytes 62914560 | tf_op jit(solution)/vmap(transpose(jvp()))/dot_general | solution.py:9
  321.9 19.4 %fusion.46 = f32[1,768,3072]{2,1,0:T(8,128)} fusion(bf16[2048,3072]{1,0:T(8,128)(2,1)} %copy-done.1, f32[2048,3072]{1,0:T(8,128)} %fusion.58, bf16[1,1,2048,768]{2,3,1,0:T(8,128)(2,1)S(1)} %copy-done.12, f32[2048]{0:T(1024)S(1)} %bitcast.308), kind=kOutput, calls=%fused_computation.69 | convolution fusion | flops 9706143744 | bytes 50339840 | tf_op jit(solution)/vmap(transpose(jvp()))/dot_general | solution.py:21
  341.5 13.2 %convolution_convert_fusion = bf16[2048,3072]{1,0:T(8,128)(2,1)S(1)} fusion(bf16[1,3072,768]{2,1,0:T(8,128)(2,1)} %all-gather.34.cloned.1.call-done, bf16[1,1,2048,768]{2,3,1,0:T(8,128)(2,1)} %copy-done.8), kind=kOutput, calls=%fused_computation.41 | convolution fusion | flops 9669967872 | bytes 20447232 | tf_op jit(solution)/vmap(transpose(jvp()))/dot_general | solution.py:9
  354.7 22.9 %fusion.7 = bf16[2048,3072]{1,0:T(8,128)(2,1)S(1)} fusion(f32[2048,3072]{1,0:T(8,128)} %fusion.68, f32[2048,3072]{1,0:T(8,128)} %fusion.64, bf16[2048,3072]{1,0:T(8,128)(2,1)S(1)} %convolution_convert_fusion), kind=kLoop, calls=%fused_computation.13 | loop fusion | flops 75497472 | bytes 75497472
  395.0 18.1 %fusion.38 = (f32[2048]{0:T(1024)S(1)}, bf16[2048,768]{0,1:T(8,128)(2,1)}) fusion(bf16[1,2048,768]{1,2,0:T(8,128)(2,1)} %copy.1, bf16[2048,768]{0,1:T(8,128)(2,1)} %fusion.70, bf16[1,768,3072]{2,1,0:T(8,128)(2,1)} %all-gather.32.cloned.1.call-done, bf16[2048,3072]{1,0:T(8,128)(2,1)S(1)} %convolution_convert_fusion, f32[2048,3072]{1,0:T(8,128)} %fusion.68), kind=kOutput, calls=%fused_computation.60 | convolution fusion | flops 9710860288 | bytes 51912704 | tf_op jit(solution)/vmap(transpose(jvp()))/dot_general | solution.py:21
  413.1 20.1 %fusion.49 = f32[1,768,3072]{2,1,0:T(8,128)} fusion(bf16[2048,3072]{1,0:T(8,128)(2,1)} %copy-done.3, f32[2048,3072]{1,0:T(8,128)} %fusion.68, bf16[1,2048,768]{1,2,0:T(8,128)(2,1)} %copy.1, f32[2048]{0:T(1024)S(1)} %bitcast.310), kind=kOutput, calls=%fused_computation.70 | convolution fusion | flops 9706143744 | bytes 50339840 | tf_op jit(solution)/vmap(transpose(jvp()))/dot_general | solution.py:21
  435.1 15.0 %convolution_bitcast_fusion.2 = f32[1,768,3072]{2,1,0:T(8,128)} fusion(bf16[2048,3072]{1,0:T(8,128)(2,1)} %copy-done, bf16[1,1,2048,768]{2,3,1,0:T(8,128)(2,1)S(1)} %copy-done.13, f32[2048]{0:T(1024)S(1)} %bitcast.309), kind=kOutput, calls=%fused_computation.67 | convolution fusion | flops 9668395008 | bytes 25174016 | tf_op jit(solution)/vmap(transpose(jvp()))/dot_general | solution.py:20
  452.0 15.2 %convolution_bitcast_fusion.1 = f32[1,768,3072]{2,1,0:T(8,128)} fusion(bf16[2048,3072]{1,0:T(8,128)(2,1)} %copy-done.2, bf16[1,2048,768]{1,2,0:T(8,128)(2,1)S(1)} %copy-done.6, f32[2048]{0:T(1024)S(1)} %bitcast.311), kind=kOutput, calls=%fused_computation.66 | convolution fusion | flops 9668395008 | bytes 25174016 | tf_op jit(solution)/vmap(transpose(jvp()))/dot_general | solution.py:20
  483.8 30.3 %reduce-scatter.25.cloned.1.call-done = f32[1,96,3072]{2,1,0:T(8,128)} async-done(((f32[1,768,3072]{2,1,0:T(8,128)}), f32[1,96,3072]{2,1,0:T(8,128)}) %reduce-scatter.25.cloned.1.call-update) | async-done | bytes 1179664
  516.5 53.0 %reduce-scatter.19.cloned.1.call-done = f32[1,96,3072]{2,1,0:T(8,128)} async-done(((f32[1,768,3072]{2,1,0:T(8,128)}), f32[1,96,3072]{2,1,0:T(8,128)}) %reduce-scatter.19.cloned.1.call-update) | async-done | bytes 1179664
  570.8 53.9 %reduce-scatter.21.cloned.1.call-done = f32[1,96,3072]{2,1,0:T(8,128)} async-done(((f32[1,768,3072]{2,1,0:T(8,128)}), f32[1,96,3072]{2,1,0:T(8,128)}) %reduce-scatter.21.cloned.1.call-update) | async-done | bytes 1179664
  (89 shorter events, 111.6 us)
Async XLA Ops:
  7.2 9.5 %copy-start.4 = (bf16[1,2048,768]{2,1,0:T(8,128)(2,1)S(1)}, bf16[1,2048,768]{2,1,0:T(8,128)(2,1)}, u32[]{:S(2)}) copy-start(bf16[1,2048,768]{2,1,0:T(8,128)(2,1)} %param.1) | copy-start | bytes 9437188
  7.2 35.5 %all-gather.30.cloned.1.call-start = ((), (), s32[]{:S(2)}) async-start(), calls=%async_computation.6 | async-start | bytes 5308416 | tf_op jit(solution)/vmap(jvp())/squeeze | solution.py:27
  9.8 64.9 %all-gather.32.cloned.1.call-start = ((), (), s32[]{:S(2)}) async-start(), calls=%async_computation.7 | async-start | bytes 5308416 | tf_op jit(solution)/vmap(jvp())/squeeze | solution.py:27
  12.3 100.3 %all-gather.34.cloned.1.call-start = ((), (), s32[]{:S(2)}) async-start(), calls=%async_computation.8 | async-start | bytes 5308416 | tf_op jit(solution)/vmap(jvp())/squeeze | solution.py:27
  14.7 123.5 %all-gather.36.cloned.1.call-start = ((), (), s32[]{:S(2)}) async-start(), calls=%async_computation.9 | async-start | bytes 5308416 | tf_op jit(solution)/vmap(jvp())/squeeze | solution.py:27
  15.4 154.8 %all-gather.40.cloned.1.call-start = ((), (), s32[]{:S(2)}) async-start(), calls=%async_computation.11 | async-start | bytes 5308416 | tf_op jit(solution)/vmap(jvp())/squeeze | solution.py:27
  16.0 185.5 %all-gather.38.cloned.1.call-start = ((), (), s32[]{:S(2)}) async-start(), calls=%async_computation.10 | async-start | bytes 5308416 | tf_op jit(solution)/vmap(jvp())/squeeze | solution.py:27
  16.6 462.0 %reduce-scatter.29.cloned.1.call-start = ((), (), s32[]{:S(2)}) async-start(), calls=%async_computation.17 | async-start | bytes 10616832
  90.6 21.9 %copy-start.5 = (bf16[1,2048,768]{1,2,0:T(8,128)(2,1)S(1)}, bf16[1,2048,768]{1,2,0:T(8,128)(2,1)}, u32[]{:S(2)}) copy-start(bf16[1,2048,768]{1,2,0:T(8,128)(2,1)} %copy.1) | copy-start | bytes 9437188
  128.7 191.5 %copy-start.14 = (f32[1,1,2048]{2,1,0:T(1,128)}, f32[1,1,2048]{2,1,0:T(1,128)S(1)}, u32[]{:S(2)}) copy-start(f32[1,1,2048]{2,1,0:T(1,128)S(1)} %rsqrt.23) | copy-start | bytes 24580
  138.2 31.9 %copy-start.10 = (bf16[1,1,2048,768]{2,3,1,0:T(8,128)(2,1)S(1)}, bf16[1,1,2048,768]{2,3,1,0:T(8,128)(2,1)}, u32[]{:S(2)}) copy-start(bf16[1,1,2048,768]{2,3,1,0:T(8,128)(2,1)} %get-tuple-element.15) | copy-start | bytes 9437188
  214.6 40.2 %copy-start.1 = (bf16[2048,3072]{1,0:T(8,128)(2,1)}, bf16[2048,3072]{1,0:T(8,128)(2,1)S(1)}, u32[]{:S(2)}) copy-start(bf16[2048,3072]{1,0:T(8,128)(2,1)S(1)} %convolution_convert_fusion.1) | copy-start | bytes 37748740
  237.4 4.5 copy-start
  254.7 18.0 %copy-start.7 = (bf16[1,2048,768]{1,2,0:T(8,128)(2,1)S(1)}, bf16[1,2048,768]{1,2,0:T(8,128)(2,1)}, u32[]{:S(2)}) copy-start(bf16[1,2048,768]{1,2,0:T(8,128)(2,1)} %copy) | copy-start | bytes 9437188
  254.7 18.0 %copy-start.11 = (bf16[1,1,2048,768]{2,3,1,0:T(8,128)(2,1)S(1)}, bf16[1,1,2048,768]{2,3,1,0:T(8,128)(2,1)}, u32[]{:S(2)}) copy-start(bf16[1,1,2048,768]{2,3,1,0:T(8,128)(2,1)} %get-tuple-element.15) | copy-start | bytes 9437188
  294.4 185.6 %reduce-scatter.27.cloned.1.call-start = ((), (), s32[]{:S(2)}) async-start(), calls=%async_computation.16 | async-start | bytes 10616832
  320.1 162.3 %reduce-scatter.23.cloned.1.call-start = ((), (), s32[]{:S(2)}) async-start(), calls=%async_computation.14 | async-start | bytes 10616832
  341.4 172.7 %reduce-scatter.25.cloned.1.call-start = ((), (), s32[]{:S(2)}) async-start(), calls=%async_computation.15 | async-start | bytes 10616832
  354.7 40.2 %copy-start.3 = (bf16[2048,3072]{1,0:T(8,128)(2,1)}, bf16[2048,3072]{1,0:T(8,128)(2,1)S(1)}, u32[]{:S(2)}) copy-start(bf16[2048,3072]{1,0:T(8,128)(2,1)S(1)} %convolution_convert_fusion) | copy-start | bytes 37748740
  377.6 4.6 copy-start.2
  395.0 18.1 %copy-start.16 = (f32[2048]{0:T(1024)S(1)}, f32[2048]{0:T(1024)}, u32[]{:S(2)}) copy-start(f32[2048]{0:T(1024)} %get-tuple-element.12) | copy-start | bytes 24580
  433.2 1.9 copy-start.15
  433.3 136.2 %reduce-scatter.19.cloned.1.call-start = ((), (), s32[]{:S(2)}) async-start(), calls=%async_computation.12 | async-start | bytes 10616832
  450.2 174.5 %reduce-scatter.21.cloned.1.call-start = ((), (), s32[]{:S(2)}) async-start(), calls=%async_computation.13 | async-start | bytes 10616832
  (5 other events, 9.2 us)
Sparse Core Ops, SparseCore 0:
  9.9 32.6 all-gather.29
  44.8 29.9 all-gather.31
  76.3 29.9 all-gather.33
  108.3 29.9 all-gather.35
  140.2 29.8 all-gather.39
  171.6 29.8 all-gather.37
  294.5 53.4 reduce-scatter.28
  350.3 53.0 reduce-scatter.26
  405.7 53.0 reduce-scatter.22
  461.0 53.0 reduce-scatter.24
  516.4 53.0 reduce-scatter.18
  571.6 53.0 reduce-scatter.20
where the time goes:
time: 644 us; the launch traced here: 634 us
  matrix products  279 us (43%)
  waiting for transfers between devices  212 us (33%)
  other arithmetic  91.1 us (14%)
  local copies, waits for them, and re-layouts  37.1 us (6%)
  between operations  14.9 us (2%)
    unnamed x18, waiting for transfers between devices  139 us
    dot_general x6, matrix products, layer(): up = jnp.dot(a, w['w_up'], preferred_element_type=jnp.float32)  107 us
    dot_general x6, matrix products, layer(): gate = jnp.dot(a, w['w_gate'], preferred_element_type=jnp.float32)  89.6 us
    dot_general x5, matrix products, matmul(): jnp.dot(a, w, preferred_element_type=jnp.float32).astype(jnp.bfloat16)  82 us
    squeeze x6, waiting for transfers between devices, stack(): h = layer(h, {name: w[number] for name, w in weights.items()})  72.4 us
    unnamed x3, other arithmetic  67.6 us
    unnamed x37, local copies, waits for them, and re-layouts  30 us
  transfers between devices with their start and end apart: 12, of which 8 were waited for; matrix products, arithmetic and copies ran while one was open for 47% of the time, Pallas kernels for 0%

commit v1 on v0

v1 whole, which is shorter than its diff:
```python
import functools

import jax
import jax.numpy as jnp
from jax import lax
from jax.experimental import pallas as pl
from jax.experimental.pallas import tpu as pltpu
from jax.sharding import PartitionSpec as P

MESH = pl.DeviceIdType.MESH
F32, BF16 = jnp.float32, jnp.bfloat16
LANES = 128
NT = (((1,), (1,)), ((), ()))
G, U, D = range(3)


def dot(a, b, dims=(((1,), (0,)), ((), ()))):
    return lax.dot_general(a, b, dims, preferred_element_type=F32)


def loop(n, body, unroll=1):
    def step(i, carry):
        body(i)
        return carry

    lax.fori_loop(0, n, step, 0, unroll=unroll)


def kernel(size, x_hbm, dy_hbm, wg_hbm, wu_hbm, wd_hbm,
           dx_hbm, og_hbm, ou_hbm, od_hbm, fg, fu, fd,
           own_g, own_u, own_d, sg, su, sd, h, a, at, dout, dt, da, act, dg, du,
           pg, pu, pd, sib_g, sib_u, sib_d, send_a_g, send_a_d, send_b_g, send_b_d,
           ra_g, ra_d, rb_g, rb_d, out_g, out_d,
           ag_send, ag_recv, own_sem, own_out, slot_sem, in_sem,
           sib_send, sib_recv, a_send, a_recv, b_send, b_recv, out_sem, credit):
    layers, chunks, rows, d, ff_chunk, tokens = (
        size[k] for k in ("layers", "chunks", "rows", "d", "ff_chunk", "tokens"))
    n = size["n"]
    chips = n // 2
    me = lax.axis_index("dp")
    x, c = me // 2, me % 2
    xr, xl, xo = lax.rem(x + 1, chips), lax.rem(x + chips - 1, chips), lax.rem(x + 2, chips)
    right, left, sibling = {"dp": xr * 2 + c}, {"dp": xl * 2 + c}, {"dp": x * 2 + 1 - c}
    units = layers * chunks

    barrier = pltpu.get_barrier_semaphore()
    for who in (left, right, sibling):
        pl.semaphore_signal(barrier, inc=1, device_id=who, device_id_type=MESH)

    R = (rows, rows, LANES)
    own, full, slot = (own_g, own_u, own_d), (fg, fu, fd), (sg, su, sd)

    def own_copies(q, m):
        l, k = q // chunks, q % chunks
        if m == D:
            return [pltpu.make_async_copy(wd_hbm.at[l, pl.ds(k * LANES, LANES)], own_d.at[q], own_sem.at[m, q, 0])]
        src = (wg_hbm, wu_hbm)[m]
        return [pltpu.make_async_copy(
            src.at[l, :, pl.ds((j * chunks + k) * LANES, LANES)], own[m].at[q, :, pl.ds(j * LANES, LANES)],
            own_sem.at[m, q, j]) for j in range(n)]

    def load_x(dst):
        return pltpu.make_async_copy(x_hbm.at[0], dst, in_sem.at[0])

    load_dy = pltpu.make_async_copy(dy_hbm.at[0], dout, in_sem.at[1])
    for q in range(units):
        for m in range(3):
            for cp in own_copies(q, m):
                cp.start()
        if q == 0:
            load_x(h).start()
            load_dy.start()

    def block(q, m, owner, half=None):
        start, size_ = owner * R[m], R[m]
        if half is not None:
            size_ = R[m] // 2
            start = start + half * size_
        return full[m].at[q, pl.ds(pl.multiple_of(start, 16), size_)]

    def remote(q, m, i, src, dst, to):
        return pltpu.make_async_remote_copy(src, dst, ag_send.at[q, m, i], ag_recv.at[q, m, i],
                                            device_id=to, device_id_type=MESH)

    def gather_copy(q, m, i):
        to = (right, left, sibling, right, sibling, left, sibling, sibling)[i]
        if i < 3:
            return remote(q, m, i, own[m].at[q], block(q, m, me), to)
        chip, half = ((xl, 0), (xl, None), (xr, 1), (xr, None), (xo, None))[i - 3]
        piece = block(q, m, chip * 2 + c, half)
        return remote(q, m, i, piece, piece, to)

    def own_store(q, m):
        return pltpu.make_async_copy(own[m].at[q], block(q, m, me), own_out.at[m, q])

    def g0(q, m):
        for i in range(3):
            gather_copy(q, m, i).start()
        own_store(q, m).start()

    def g1(q, m):
        for came in range(2):
            gather_copy(q, m, came).wait_recv()
            gather_copy(q, m, 3 + 2 * came).start()
            gather_copy(q, m, 4 + 2 * came).start()

    def g2(q, m):
        gather_copy(q, m, 3).wait_recv()
        gather_copy(q, m, 5).wait_recv()
        gather_copy(q, m, 7).start()

    def g3(q, m):
        for i in (2, 4, 6, 7):
            gather_copy(q, m, i).wait_recv()
        own_store(q, m).wait()

    def g_end(q, m):
        for i in range(8):
            gather_copy(q, m, i).wait_send()

    def fetch(q, s, m):
        return pltpu.make_async_copy(full[m].at[q], slot[m].at[s], slot_sem.at[s, m])

    TP = 256
    prep_tiles = tokens // TP

    def scale_of(wide):
        return lax.rsqrt(jnp.mean(wide * wide, -1, keepdims=True) + 1e-6)

    def norm_tile(i):
        r = pl.ds(i * TP, TP)
        wide = h[r, :].astype(F32)
        a_tile = (wide * scale_of(wide)).astype(BF16)
        a[r, :] = a_tile
        return a_tile

    def transpose_a(i):
        cols = pl.ds(pl.multiple_of(i * TP, TP), TP)
        at[:, cols] = norm_tile(i).T

    def transpose_dout(i):
        cols = pl.ds(pl.multiple_of(i * TP, TP), TP)
        dt[:, cols] = dout[pl.ds(i * TP, TP), :].T

    T, NB = 512, 256
    tiles, blocks = tokens // T, ff_chunk // NB

    def forward_tile(s, i, first):
        r = pl.ds(i * T, T)
        a_tile = a[r, :]
        gate = dot(a_tile, sg[s])
        up = dot(a_tile, su[s])
        hidden = (gate * jax.nn.sigmoid(gate) * up).astype(BF16)
        term = dot(hidden, sd[s])

        @pl.when(first)
        def _():
            da[r, :] = term

        @pl.when(jnp.logical_not(first))
        def _():
            da[r, :] += term

    def hidden_tile(s, i):
        r = pl.ds(pl.multiple_of((i % tiles) * T, T), T)
        f = pl.ds(pl.multiple_of((i // tiles) * NB, NB), NB)
        a_tile = a[r, :]
        gate = dot(a_tile, sg[s, :, f])
        up = dot(a_tile, su[s, :, f])
        by_hidden = dot(dout[r, :], sd[s, f, :], NT).astype(BF16).astype(F32)
        sig = jax.nn.sigmoid(gate)
        silu = gate * sig
        act[r, f] = (silu * up).astype(BF16)
        du[r, f] = (by_hidden * silu).astype(BF16)
        dg[r, f] = (by_hidden * up * (sig + silu * (1.0 - sig))).astype(BF16)

    def weights_up(b, src, dst):
        f = pl.ds(pl.multiple_of(b * NB, NB), NB)
        term = dot(at[...], src[:, f]).astype(BF16)
        dst[:, :, f] = term.reshape(chips, 2 * rows, NB)

    def weights_down(b):
        f = pl.ds(pl.multiple_of(b * NB, NB), NB)
        term = dot(dt[...], act[:, f])
        pd[b] = term.T.astype(BF16)

    def input_tile(s, i, first):
        r = pl.ds(i * T, T)
        term = dot(dg[r, :], sg[s], NT) + dot(du[r, :], su[s], NT)

        @pl.when(first)
        def _():
            da[r, :] = term

        @pl.when(jnp.logical_not(first))
        def _():
            da[r, :] += term

    def norm_back(i):
        r = pl.ds(i * TP, TP)
        wide = h[r, :].astype(F32)
        s = scale_of(wide)
        g = da[r, :].astype(BF16).astype(F32)
        along = jnp.sum(g * wide, -1, keepdims=True)
        back = (g * s - wide * (s * s * s * along * (1.0 / d))).astype(BF16)
        dout[r, :] = (dout[r, :].astype(F32) + back.astype(F32)).astype(BF16)

    part, sib = (pg, pu, pd), (sib_g, sib_u, sib_d)
    view = lambda pair, m: pair[0].at[m] if m != D else pair[1]
    sa = [view((send_a_g, send_a_d), m) for m in range(3)]
    ra = [[r_.at[i] for i in range(2)] for r_ in (view((ra_g, ra_d), m) for m in range(3))]
    sb = [[r_.at[i] for i in range(2)] for r_ in (view((send_b_g, send_b_d), m) for m in range(3))]
    rb = [[r_.at[i] for i in range(2)] for r_ in (view((rb_g, rb_d), m) for m in range(3))]
    out = [view((out_g, out_d), m) for m in range(3)]

    def rs_sib(m):
        return pltpu.make_async_remote_copy(
            part[m].at[:, pl.ds(pl.multiple_of((1 - c) * R[m], 16), R[m])], sib[m], sib_send.at[m], sib_recv.at[m],
            device_id=sibling, device_id_type=MESH)

    def rs_a(m, i):
        half = R[m] // 2
        return pltpu.make_async_remote_copy(
            sa[m].at[pl.ds(i * half, half)], ra[m][i], a_send.at[m, i], a_recv.at[m, i],
            device_id=(right, left)[i], device_id_type=MESH)

    def rs_b(m, i):
        return pltpu.make_async_remote_copy(
            sb[m][i], rb[m][i], b_send.at[m, i], b_recv.at[m, i],
            device_id=(right, left)[i], device_id_type=MESH)

    def term(m, chip):
        mine = part[m][chip, pl.ds(pl.multiple_of(c * R[m], 16), R[m]), :]
        return mine.astype(F32) + sib[m][chip].astype(F32)

    def rs1(s, m):
        @pl.when(s > 0)
        def _():
            pl.semaphore_wait(credit.at[m], 1)

        rs_sib(m).start()

    def rs2(s, m):
        rs_sib(m).wait()
        sa[m][...] = term(m, xo).astype(BF16)
        for i in range(2):
            rs_a(m, i).start()

    def rs3(m):
        half = R[m] // 2
        for i in range(2):
            rs_a(m, i).wait()
        for i, chip in enumerate((xr, xl)):
            whole = term(m, chip)
            came = ra[m][i][...].astype(F32)
            top, low = whole[:half], whole[half:]
            if i == 0:
                top = top + came
            else:
                low = low + came
            sb[m][i][:half, :] = top.astype(BF16)
            sb[m][i][half:, :] = low.astype(BF16)
        for i in range(2):
            rs_b(m, i).start()

    def out_copies(s, m):
        l, k = layers - 1 - s // chunks, lax.rem(s, chunks)
        if m == D:
            return [pltpu.make_async_copy(out[m], od_hbm.at[l, pl.ds(k * LANES, LANES)], out_sem.at[m, 0])]
        dst = (og_hbm, ou_hbm)[m]
        return [pltpu.make_async_copy(
            out[m].at[:, pl.ds(j * LANES, LANES)],
            dst.at[l, :, pl.ds(pl.multiple_of((j * chunks + k) * LANES, LANES), LANES)], out_sem.at[m, j])
            for j in range(n)]

    def rs4(s, m):
        @pl.when(s > 0)
        def _():
            for cp in out_copies(s, m):
                cp.wait()

        for i in range(2):
            rs_b(m, i).wait()
        total = term(m, x) + rb[m][0][...].astype(F32) + rb[m][1][...].astype(F32)
        out[m][...] = total.astype(BF16)
        for cp in out_copies(s, m):
            cp.start()

        @pl.when(s < units - 1)
        def _():
            pl.semaphore_signal(credit.at[m], inc=1, device_id=sibling, device_id_type=MESH)

    for m in range(3):
        for cp in own_copies(0, m):
            cp.wait()
    pl.semaphore_wait(barrier, 3)
    for m in range(3):
        g0(0, m)
    for q in range(1, units):
        for m in range(3):
            for cp in own_copies(q, m):
                cp.wait()
    load_x(h).wait()
    loop(prep_tiles, norm_tile)
    load_dy.wait()
    loop(prep_tiles, transpose_dout)

    def finish_gather(q, s):
        for m in range(3):
            g2(q, m)
        for m in range(3):
            g3(q, m)
            fetch(q, s, m).start()

    for m in range(3):
        g1(0, m)
    for m in range(3):
        g0(1, m)
    finish_gather(0, 0)

    def forward(k, carry):
        s = lax.rem(k, 2)
        for m in range(3):
            fetch(k, s, m).wait()

        def tile(i):
            for m in range(2):
                @pl.when(i == 1 + 2 * m)
                def _():
                    g1(k + 1, m)

            forward_tile(s, i, k == 0)

        loop(tiles, tile)
        g1(k + 1, D)
        for m in range(3):
            g0(k + 2, m)
        finish_gather(k + 1, lax.rem(k + 1, 2))
        return carry

    fwd = units - chunks
    lax.fori_loop(0, fwd, forward, 0)

    def add_hidden(i):
        r = pl.ds(i * TP, TP)
        h[r, :] = (h[r, :].astype(F32) + da[r, :].astype(BF16).astype(F32)).astype(BF16)

    loop(prep_tiles, add_hidden)
    loop(prep_tiles, transpose_a)

    def backward(k, carry):
        s = lax.rem(k + fwd, 2)
        q_next = lax.rem(k + fwd + 1, units)
        more = k < units - fwd - 1
        first = lax.rem(k, chunks) == 0

        @pl.when(jnp.logical_and(first, k > 0))
        def _():
            load_x(h).wait()
            loop(prep_tiles, transpose_a)
            loop(prep_tiles, transpose_dout)

        @pl.when(k > 0)
        def _():
            for m in range(3):
                rs3(m)

        for m in range(3):
            fetch(0, s, m).wait()

        def tile(i):
            for m in range(3):
                @pl.when(jnp.logical_and(more, i == 1 + 6 * m))
                def _():
                    g1(q_next, m)

            hidden_tile(s, i)

        loop(tiles * blocks, tile)

        @pl.when(k < units - fwd - 2)
        def _():
            for m in range(3):
                g0(q_next + 1, m)

        @pl.when(k > 0)
        def _():
            for m in range(3):
                rs4(k - 1, m)

        loop(blocks, lambda b: weights_up(b, dg, pg))
        rs1(k, G)
        loop(blocks, lambda b: weights_up(b, du, pu))
        rs1(k, U)
        rs2(k, G)

        @pl.when(more)
        def _():
            for m in range(3):
                g2(q_next, m)

        loop(blocks, weights_down)
        rs1(k, D)
        rs2(k, U)

        @pl.when(more)
        def _():
            for m in range(3):
                g3(q_next, m)

        @pl.when(k < units - 1)
        def _():
            for m in range(3):
                fetch(q_next, 1 - s, m).start()

        def back(i):
            @pl.when(i == 1)
            def _():
                rs2(k, D)

            input_tile(s, i, first)

        loop(tiles, back)

        @pl.when(lax.rem(k, chunks) == chunks - 1)
        def _():
            loop(prep_tiles, norm_back)

            @pl.when(k < units - 1)
            def _():
                load_x(h).start()

        return carry

    lax.fori_loop(0, units, backward, 0)
    store_dx = pltpu.make_async_copy(dout, dx_hbm.at[0], in_sem.at[1])
    store_dx.start()
    for m in range(3):
        rs3(m)
    for m in range(3):
        rs4(units - 1, m)
    for m in range(3):
        for cp in out_copies(units - 1, m):
            cp.wait()
    store_dx.wait()

    def ends(q):
        for m in range(3):
            g_end(q, m)

    loop(units, ends)


def solution(mesh):
    n = mesh.shape["dp"]

    def step(x, dy, wg, wu, wd):
        layers, rows, ff = wg.shape
        tokens, d = x.shape[1:]
        chunks = ff // (n * LANES)
        ff_chunk = n * LANES
        units = layers * chunks
        chips = n // 2
        size = dict(layers=layers, chunks=chunks, rows=rows, d=d, ff_chunk=ff_chunk, tokens=tokens, n=n)
        sds = jax.ShapeDtypeStruct
        vm = pltpu.VMEM
        dma = pltpu.SemaphoreType.DMA
        hbm = pl.BlockSpec(memory_space=pl.ANY)
        td = (tokens, d)
        tf = (tokens, ff_chunk)
        up, down = (rows, ff_chunk), (LANES, d)
        scratch = [
            vm((units, *up), BF16), vm((units, *up), BF16), vm((units, *down), BF16),
            vm((2, d, ff_chunk), BF16), vm((2, d, ff_chunk), BF16), vm((2, ff_chunk, d), BF16),
            vm(td, BF16), vm(td, BF16), vm(td[::-1], BF16), vm(td, BF16), vm(td[::-1], BF16), vm(td, F32),
            vm(tf, BF16), vm(tf, BF16), vm(tf, BF16),
            vm((chips, 2 * rows, ff_chunk), BF16), vm((chips, 2 * rows, ff_chunk), BF16), vm((chips, 2 * LANES, d), BF16),
            vm((chips, *up), BF16), vm((chips, *up), BF16), vm((chips, *down), BF16),
            vm((2, *up), BF16), vm(down, BF16), vm((2, 2, *up), BF16), vm((2, *down), BF16),
            vm((2, 2, rows // 2, ff_chunk), BF16), vm((2, LANES // 2, d), BF16), vm((2, 2, *up), BF16), vm((2, *down), BF16),
            vm((2, *up), BF16), vm(down, BF16),
            dma((units, 3, 8)), dma((units, 3, 8)), dma((3, units, n)), dma((3, units)), dma((2, 3)), dma((2,)),
            dma((3,)), dma((3,)), dma((3, 2)), dma((3, 2)), dma((3, 2)), dma((3, 2)), dma((3, n)),
            pltpu.SemaphoreType.REGULAR((3,)),
        ]
        outs = pl.pallas_call(
            functools.partial(kernel, size),
            out_shape=[
                sds(x.shape, BF16), sds(wg.shape, BF16), sds(wu.shape, BF16), sds(wd.shape, BF16),
                sds((units, d, ff_chunk), BF16), sds((units, d, ff_chunk), BF16), sds((units, ff_chunk, d), BF16),
            ],
            in_specs=[hbm] * 5,
            out_specs=[hbm] * 7,
            scratch_shapes=scratch,
            compiler_params=pltpu.CompilerParams(
                collective_id=0, has_side_effects=True, vmem_limit_bytes=67_043_328),
            name="stack",
        )(x, dy, wg, wu, wd)
        return tuple(outs[:4])

    seq, w = P(("rep", "dp"), None, None), P(None, "dp", None)
    return jax.shard_map(step, mesh=mesh, in_specs=(seq, seq, w, w, w),
                         out_specs=(seq, *(P("rep", "dp", None),) * 3), check_vma=False)
```

time: 644 us -> 347 us (0.54); the launches traced: 634 us -> 347 us
  Pallas kernels: 0 us -> 338 us
  matrix products: 279 us -> 0 us
  waiting for transfers between devices: 212 us -> 0 us
  other arithmetic: 91.1 us -> 0 us
  local copies, waits for them, and re-layouts: 37.1 us -> 8.26 us
  between operations: 14.9 us -> 0.65 us
    pallas_call x0 -> x1, Pallas kernels: none -> 338 us  [step(): pl.pallas_call(functools.partial(kernel, size), out_shape=[sds(x.shape, B...]
    dot_general x17 -> x0, matrix products: 279 us -> none  [the longest x6 107 us: layer(): up = jnp.dot(a, w['w_up'], preferred_element_type=jnp.float32)]
    unnamed x18 -> x0, waiting for transfers between devices: 139 us -> none
    squeeze x6 -> x0, waiting for transfers between devices: 72.4 us -> none  [stack(): h = layer(h, {name: w[number] for name, w in weights.items()})]
    unnamed x3 -> x0, other arithmetic: 67.6 us -> none
    unnamed x37 -> x10, local copies, waits for them, and re-layouts: 30 us -> 8.26 us
    reshape x4 -> x0, other arithmetic: 9.97 us -> none  [the longest x1 6.69 us: step(): by_x.reshape(shape)]
    broadcast_in_dim x6 -> x0, other arithmetic: 7.99 us -> none  [stack(): h = layer(h, {name: w[number] for name, w in weights.items()})]
  transfers between devices with their start and end apart: 12 -> 0, of which waited for: 8 -> 0; matrix products, arithmetic and copies ran while one was open for 47% -> 0% of each run, Pallas kernels for 0% -> 0%
where the time goes in v1:
time: 347 us
  Pallas kernels  338 us (97%)
  local copies, waits for them, and re-layouts  8.26 us (2%)
    pallas_call x1, Pallas kernels, step(): pl.pallas_call(functools.partial(kernel, size), out_shape=[sds(x.shape, B...  338 us
    unnamed x10, local copies, waits for them, and re-layouts  8.26 us

profile of v1, /device:TPU:112, one launch (start us, length us, event | category | flops | bytes accessed | tf_op | source)
XLA Modules:
  0.0 347.0 jit_solution(3373252664991167191)
XLA Ops:
  0.6 338.1 %stack.1 = (bf16[1,2048,768]{2,1,0:T(8,128)(2,1)}, bf16[2,96,3072]{2,1,0:T(8,128)(2,1)}, bf16[2,96,3072]{2,1,0:T(8,128)(2,1)}, bf16[2,384,768]{2,1,0:T(8,128)(2,...) custom-call(bf16[1,2048,768]{2,1,0:T(8,128)(2,1)} %x_hbm.1, ...), custom_call_target="tpu_custom_call" | custom-call | tf_op jit(solution)/shard_map/stack/pallas_call | solution.py:486
  338.7 0.0 copy-start.2
  338.7 3.9 %copy.13 = bf16[1,2048,768]{2,1,0:T(8,128)(2,1)} copy(bf16[1,2048,768]{2,1,0:T(8,128)(2,1)} %get-tuple-element.16) | data formatting | bytes 6291456
  342.6 0.0 copy-done.2
  342.6 0.0 copy-start.1
  342.6 1.0 copy.14
  343.6 0.7 copy-done.1
  344.3 0.0 copy-start
  344.3 1.0 copy.15
  345.3 0.7 copy-done
  346.0 1.0 copy.16
Async XLA Ops:
  338.7 3.9 %copy-start.2 = (bf16[2,96,3072]{2,1,0:T(8,128)(2,1)S(1)}, bf16[2,96,3072]{2,1,0:T(8,128)(2,1)}, u32[]{:S(2)}) copy-start(bf16[2,96,3072]{2,1,0:T(8,128)(2,1)} %get-tuple-element.17) | copy-start | bytes 3538948
  342.6 1.7 copy-start.1
  344.3 1.7 copy-start

commit v2 on v1

--- a/solution.py
+++ b/solution.py
@@ -28,7 +28,7 @@
 
 def kernel(size, x_hbm, dy_hbm, wg_hbm, wu_hbm, wd_hbm,
            dx_hbm, og_hbm, ou_hbm, od_hbm, fg, fu, fd,
-           own_g, own_u, own_d, sg, su, sd, h, a, at, dout, dt, da, act, dg, du,
+           own_g, own_u, own_d, sgu, sd, h, a, at, dout, dt, da, act, dgu,
            pg, pu, pd, sib_g, sib_u, sib_d, send_a_g, send_a_d, send_b_g, send_b_d,
            ra_g, ra_d, rb_g, rb_d, out_g, out_d,
            ag_send, ag_recv, own_sem, own_out, slot_sem, in_sem,
@@ -44,11 +44,15 @@
     units = layers * chunks
 
     barrier = pltpu.get_barrier_semaphore()
-    for who in (left, right, sibling):
+    other = {"rep": lax.axis_index("rep") + 1 - 2 * (lax.axis_index("rep") % 2)}
+    for who in (left, right, sibling, other):
         pl.semaphore_signal(barrier, inc=1, device_id=who, device_id_type=MESH)
 
     R = (rows, rows, LANES)
-    own, full, slot = (own_g, own_u, own_d), (fg, fu, fd), (sg, su, sd)
+    own, full = (own_g, own_u, own_d), (fg, fu, fd)
+    sg, su = (sgu.at[:, :, pl.ds(i * ff_chunk, ff_chunk)] for i in range(2))
+    dg, du = (dgu.at[:, pl.ds(i * ff_chunk, ff_chunk)] for i in range(2))
+    slot = (sg, su, sd)
 
     def own_copies(q, m):
         l, k = q // chunks, q % chunks
@@ -63,60 +67,106 @@
         return pltpu.make_async_copy(x_hbm.at[0], dst, in_sem.at[0])
 
     load_dy = pltpu.make_async_copy(dy_hbm.at[0], dout, in_sem.at[1])
-    for q in range(units):
-        for m in range(3):
-            for cp in own_copies(q, m):
-                cp.start()
-        if q == 0:
-            load_x(h).start()
-            load_dy.start()
-
-    def block(q, m, owner, half=None):
-        start, size_ = owner * R[m], R[m]
-        if half is not None:
-            size_ = R[m] // 2
-            start = start + half * size_
-        return full[m].at[q, pl.ds(pl.multiple_of(start, 16), size_)]
-
-    def remote(q, m, i, src, dst, to):
+
+    S = tuple(r // 3 // 16 * 16 for r in R)
+    pair = lax.axis_index("rep") % 2
+    partner = {"rep": lax.axis_index("rep") + 1 - 2 * pair}
+
+    def block(q, m, owner, start, count):
+        return full[m].at[q, pl.ds(pl.multiple_of(owner * R[m] + start, 16), count)]
+
+    def gather_copy(q, m, i):
+        to = (right, left, sibling, right, sibling, left, sibling, sibling,
+              partner, partner, partner, sibling, sibling, sibling)[i]
+        ours, both = pair * S[m], R[m] - S[m]
+        if i < 2:
+            src, dst = own[m].at[q, pl.ds(pl.multiple_of(ours, 16), both)], block(q, m, me, ours, both)
+        elif i == 2:
+            src, dst = own[m].at[q], block(q, m, me, 0, R[m])
+        else:
+            owner = (xl, xl, xr, xr, xo, xl, xr, xo, xl, xr, xo)[i - 3] * 2 + c
+            if i == 3:
+                piece = (ours, both // 2)
+            elif i == 5:
+                piece = (ours + both // 2, both // 2)
+            elif i < 8:
+                piece = (ours, both)
+            elif i < 11:
+                piece = (pair * both, S[m])
+            else:
+                piece = ((1 - pair) * both, S[m])
+            src = dst = block(q, m, owner, *piece)
         return pltpu.make_async_remote_copy(src, dst, ag_send.at[q, m, i], ag_recv.at[q, m, i],
                                             device_id=to, device_id_type=MESH)
 
-    def gather_copy(q, m, i):
-        to = (right, left, sibling, right, sibling, left, sibling, sibling)[i]
-        if i < 3:
-            return remote(q, m, i, own[m].at[q], block(q, m, me), to)
-        chip, half = ((xl, 0), (xl, None), (xr, 1), (xr, None), (xo, None))[i - 3]
-        piece = block(q, m, chip * 2 + c, half)
-        return remote(q, m, i, piece, piece, to)
-
     def own_store(q, m):
-        return pltpu.make_async_copy(own[m].at[q], block(q, m, me), own_out.at[m, q])
-
-    def g0(q, m):
-        for i in range(3):
-            gather_copy(q, m, i).start()
-        own_store(q, m).start()
+        return pltpu.make_async_copy(own[m].at[q], block(q, m, me, 0, R[m]), own_out.at[m, q])
+
+    def g0(q):
+        for m in range(3):
+            for i in range(3):
+                gather_copy(q, m, i).start()
+            own_store(q, m).start()
 
     def g1(q, m):
         for came in range(2):
             gather_copy(q, m, came).wait_recv()
-            gather_copy(q, m, 3 + 2 * came).start()
-            gather_copy(q, m, 4 + 2 * came).start()
+            for i in (3 + 2 * came, 8 + came, 4 + 2 * came):
+                gather_copy(q, m, i).start()
 
     def g2(q, m):
         gather_copy(q, m, 3).wait_recv()
         gather_copy(q, m, 5).wait_recv()
+        gather_copy(q, m, 10).start()
         gather_copy(q, m, 7).start()
 
     def g3(q, m):
-        for i in (2, 4, 6, 7):
-            gather_copy(q, m, i).wait_recv()
-        own_store(q, m).wait()
+        for i in range(3):
+            gather_copy_from_partner(q, m, i).wait_recv()
+            gather_copy(q, m, 11 + i).start()
+
+    def gather_copy_from_partner(q, m, i):
+        owner = (xl, xr, xo)[i] * 2 + c
+        piece = block(q, m, owner, (1 - pair) * (R[m] - S[m]), S[m])
+        return pltpu.make_async_remote_copy(piece, piece, ag_send.at[q, m, 8 + i], ag_recv.at[q, m, 8 + i],
+                                            device_id=partner, device_id_type=MESH)
+
+    def g4(q):
+        for m in range(3):
+            for i in (2, 4, 6, 7, 11, 12, 13):
+                gather_copy(q, m, i).wait_recv()
+            own_store(q, m).wait()
 
     def g_end(q, m):
-        for i in range(8):
+        for i in range(14):
             gather_copy(q, m, i).wait_send()
+
+    last = units - 1
+
+    def gather_part(q, i):
+        if i == 1:
+            @pl.when(q < last)
+            def _():
+                g1(q, D)
+                g0(q + 1)
+        elif 2 <= i < 5:
+            g2(q, i - 2)
+        elif i >= 5:
+            g3(q, i - 5)
+
+            if i == 6:
+                @pl.when(q < last)
+                def _():
+                    g1(q + 1, G)
+
+    def gather_end(q, s):
+        g4(q)
+        for m in range(3):
+            fetch(q, s, m).start()
+
+        @pl.when(q < last - 1)
+        def _():
+            g1(q + 1, U)
 
     def fetch(q, s, m):
         return pltpu.make_async_copy(full[m].at[q], slot[m].at[s], slot_sem.at[s, m])
@@ -127,9 +177,9 @@
     def scale_of(wide):
         return lax.rsqrt(jnp.mean(wide * wide, -1, keepdims=True) + 1e-6)
 
-    def norm_tile(i):
+    def norm_tile(i, src=h):
         r = pl.ds(i * TP, TP)
-        wide = h[r, :].astype(F32)
+        wide = src[r, :].astype(F32)
         a_tile = (wide * scale_of(wide)).astype(BF16)
         a[r, :] = a_tile
         return a_tile
@@ -138,11 +188,22 @@
         cols = pl.ds(pl.multiple_of(i * TP, TP), TP)
         at[:, cols] = norm_tile(i).T
 
+    def restart(i):
+        r = pl.ds(i * TP, TP)
+        cols = pl.ds(pl.multiple_of(i * TP, TP), TP)
+        h[r, :] = a[r, :]
+        at[:, cols] = norm_tile(i, a).T
+        dt[:, cols] = dout[r, :].T
+
     def transpose_dout(i):
         cols = pl.ds(pl.multiple_of(i * TP, TP), TP)
         dt[:, cols] = dout[pl.ds(i * TP, TP), :].T
 
-    T, NB = 512, 256
+    T, NB = 512, 1024
+    TI = 512
+    TH, NH = 1024, 256
+    strips = ff_chunk // NH
+    spots = strips * (tokens // TH)
     tiles, blocks = tokens // T, ff_chunk // NB
 
     def forward_tile(s, i, first):
@@ -153,17 +214,11 @@
         hidden = (gate * jax.nn.sigmoid(gate) * up).astype(BF16)
         term = dot(hidden, sd[s])
 
-        @pl.when(first)
-        def _():
-            da[r, :] = term
-
-        @pl.when(jnp.logical_not(first))
-        def _():
-            da[r, :] += term
-
-    def hidden_tile(s, i):
-        r = pl.ds(pl.multiple_of((i % tiles) * T, T), T)
-        f = pl.ds(pl.multiple_of((i // tiles) * NB, NB), NB)
+        da[r, :] = jnp.where(first, 0.0, da[r, :]) + term
+
+    def hidden_tile(s, i, b):
+        r = pl.ds(pl.multiple_of(i * TH, TH), TH)
+        f = pl.ds(pl.multiple_of(b * NH, NH), NH)
         a_tile = a[r, :]
         gate = dot(a_tile, sg[s, :, f])
         up = dot(a_tile, su[s, :, f])
@@ -182,19 +237,14 @@
     def weights_down(b):
         f = pl.ds(pl.multiple_of(b * NB, NB), NB)
         term = dot(dt[...], act[:, f])
-        pd[b] = term.T.astype(BF16)
+        per = NB // (2 * LANES)
+        pd[pl.ds(b * per, per)] = term.T.astype(BF16).reshape(per, 2 * LANES, d)
 
     def input_tile(s, i, first):
-        r = pl.ds(i * T, T)
-        term = dot(dg[r, :], sg[s], NT) + dot(du[r, :], su[s], NT)
-
-        @pl.when(first)
-        def _():
-            da[r, :] = term
-
-        @pl.when(jnp.logical_not(first))
-        def _():
-            da[r, :] += term
+        r = pl.ds(i * TI, TI)
+        term = dot(dgu[r, :], sgu[s], NT)
+
+        da[r, :] = jnp.where(first, 0.0, da[r, :]) + term
 
     def norm_back(i):
         r = pl.ds(i * TP, TP)
@@ -292,10 +342,18 @@
 
     for m in range(3):
         for cp in own_copies(0, m):
+            cp.start()
+    load_x(h).start()
+    load_dy.start()
+    for m in range(3):
+        for cp in own_copies(0, m):
             cp.wait()
-    pl.semaphore_wait(barrier, 3)
-    for m in range(3):
-        g0(0, m)
+    pl.semaphore_wait(barrier, 4)
+    g0(0)
+    for q in range(1, units):
+        for m in range(3):
+            for cp in own_copies(q, m):
+                cp.start()
     for q in range(1, units):
         for m in range(3):
             for cp in own_copies(q, m):
@@ -304,19 +362,11 @@
     loop(prep_tiles, norm_tile)
     load_dy.wait()
     loop(prep_tiles, transpose_dout)
-
-    def finish_gather(q, s):
-        for m in range(3):
-            g2(q, m)
-        for m in range(3):
-            g3(q, m)
-            fetch(q, s, m).start()
-
-    for m in range(3):
-        g1(0, m)
-    for m in range(3):
-        g0(1, m)
-    finish_gather(0, 0)
+    g1(0, G)
+    g1(0, U)
+    for i in range(8):
+        gather_part(0, i)
+    gather_end(0, 0)
 
     def forward(k, carry):
         s = lax.rem(k, 2)
@@ -324,18 +374,15 @@
             fetch(k, s, m).wait()
 
         def tile(i):
-            for m in range(2):
-                @pl.when(i == 1 + 2 * m)
+            for j in range(8):
+                @pl.when(i == j * tiles // 8)
                 def _():
-                    g1(k + 1, m)
+                    gather_part(k + 1, j)
 
             forward_tile(s, i, k == 0)
 
         loop(tiles, tile)
-        g1(k + 1, D)
-        for m in range(3):
-            g0(k + 2, m)
-        finish_gather(k + 1, lax.rem(k + 1, 2))
+        gather_end(k + 1, 1 - s)
         return carry
 
     fwd = units - chunks
@@ -356,59 +403,53 @@
 
         @pl.when(jnp.logical_and(first, k > 0))
         def _():
-            load_x(h).wait()
-            loop(prep_tiles, transpose_a)
-            loop(prep_tiles, transpose_dout)
-
-        @pl.when(k > 0)
-        def _():
-            for m in range(3):
-                rs3(m)
+            load_x(a).wait()
+            loop(prep_tiles, restart)
 
         for m in range(3):
             fetch(0, s, m).wait()
 
-        def tile(i):
-            for m in range(3):
-                @pl.when(jnp.logical_and(more, i == 1 + 6 * m))
+        def strip(b):
+            for j in range(8):
+                @pl.when(jnp.logical_and(more, b == j * strips // 8))
                 def _():
-                    g1(q_next, m)
-
-            hidden_tile(s, i)
-
-        loop(tiles * blocks, tile)
-
-        @pl.when(k < units - fwd - 2)
-        def _():
-            for m in range(3):
-                g0(q_next + 1, m)
+                    gather_part(q_next, j)
+
+            for i in range(tokens // TH):
+                hidden_tile(s, i, b)
+
+        loop(strips, strip)
 
         @pl.when(k > 0)
         def _():
             for m in range(3):
                 rs4(k - 1, m)
 
+        @pl.when(jnp.logical_and(lax.rem(k, chunks) == chunks - 1, k < units - 1))
+        def _():
+            load_x(a).start()
+
         loop(blocks, lambda b: weights_up(b, dg, pg))
         rs1(k, G)
+
+        @pl.when(jnp.logical_and(more, q_next == last - 1))
+        def _():
+            g1(last, U)
+            g1(last, D)
+
         loop(blocks, lambda b: weights_up(b, du, pu))
         rs1(k, U)
         rs2(k, G)
 
-        @pl.when(more)
-        def _():
-            for m in range(3):
-                g2(q_next, m)
-
         loop(blocks, weights_down)
         rs1(k, D)
         rs2(k, U)
 
         @pl.when(more)
         def _():
-            for m in range(3):
-                g3(q_next, m)
-
-        @pl.when(k < units - 1)
+            gather_end(q_next, 1 - s)
+
+        @pl.when(jnp.logical_and(k < units - 1, jnp.logical_not(more)))
         def _():
             for m in range(3):
                 fetch(q_next, 1 - s, m).start()
@@ -417,26 +458,27 @@
             @pl.when(i == 1)
             def _():
                 rs2(k, D)
+                rs3(G)
+
+            @pl.when(i == 2)
+            def _():
+                rs3(U)
 
             input_tile(s, i, first)
 
-        loop(tiles, back)
+        loop(tokens // TI, back)
+        rs3(D)
 
         @pl.when(lax.rem(k, chunks) == chunks - 1)
         def _():
             loop(prep_tiles, norm_back)
 
-            @pl.when(k < units - 1)
-            def _():
-                load_x(h).start()
 
         return carry
 
     lax.fori_loop(0, units, backward, 0)
     store_dx = pltpu.make_async_copy(dout, dx_hbm.at[0], in_sem.at[1])
     store_dx.start()
-    for m in range(3):
-        rs3(m)
     for m in range(3):
         rs4(units - 1, m)
     for m in range(3):
@@ -471,15 +513,15 @@
         up, down = (rows, ff_chunk), (LANES, d)
         scratch = [
             vm((units, *up), BF16), vm((units, *up), BF16), vm((units, *down), BF16),
-            vm((2, d, ff_chunk), BF16), vm((2, d, ff_chunk), BF16), vm((2, ff_chunk, d), BF16),
+            vm((2, d, 2 * ff_chunk), BF16), vm((2, ff_chunk, d), BF16),
             vm(td, BF16), vm(td, BF16), vm(td[::-1], BF16), vm(td, BF16), vm(td[::-1], BF16), vm(td, F32),
-            vm(tf, BF16), vm(tf, BF16), vm(tf, BF16),
+            vm(tf, BF16), vm((tokens, 2 * ff_chunk), BF16),
             vm((chips, 2 * rows, ff_chunk), BF16), vm((chips, 2 * rows, ff_chunk), BF16), vm((chips, 2 * LANES, d), BF16),
             vm((chips, *up), BF16), vm((chips, *up), BF16), vm((chips, *down), BF16),
             vm((2, *up), BF16), vm(down, BF16), vm((2, 2, *up), BF16), vm((2, *down), BF16),
             vm((2, 2, rows // 2, ff_chunk), BF16), vm((2, LANES // 2, d), BF16), vm((2, 2, *up), BF16), vm((2, *down), BF16),
             vm((2, *up), BF16), vm(down, BF16),
-            dma((units, 3, 8)), dma((units, 3, 8)), dma((3, units, n)), dma((3, units)), dma((2, 3)), dma((2,)),
+            dma((units, 3, 14)), dma((units, 3, 14)), dma((3, units, n)), dma((3, units)), dma((2, 3)), dma((2,)),
             dma((3,)), dma((3,)), dma((3, 2)), dma((3, 2)), dma((3, 2)), dma((3, 2)), dma((3, n)),
             pltpu.SemaphoreType.REGULAR((3,)),
         ]

time: 347 us -> 295 us (0.85)
  Pallas kernels: 338 us -> 286 us
    pallas_call x1, Pallas kernels: 338 us -> 286 us  [step(): pl.pallas_call(functools.partial(kernel, size), out_shape=[sds(x.shape, B...]
where the time goes in v2:
time: 295 us
  Pallas kernels  286 us (97%)
  local copies, waits for them, and re-layouts  8.26 us (3%)
    pallas_call x1, Pallas kernels, step(): pl.pallas_call(functools.partial(kernel, size), out_shape=[sds(x.shape, B...  286 us
    unnamed x10, local copies, waits for them, and re-layouts  8.26 us

profile of v2, /device:TPU:112, one launch (start us, length us, event | category | flops | bytes accessed | tf_op | source)
XLA Modules:
  0.0 294.8 jit_solution(16811053811071483529)
XLA Ops:
  0.6 285.8 %stack.1 = (bf16[1,2048,768]{2,1,0:T(8,128)(2,1)}, bf16[2,96,3072]{2,1,0:T(8,128)(2,1)}, bf16[2,96,3072]{2,1,0:T(8,128)(2,1)}, bf16[2,384,768]{2,1,0:T(8,128)(2,...) custom-call(bf16[1,2048,768]{2,1,0:T(8,128)(2,1)} %x_hbm.1, ...), custom_call_target="tpu_custom_call" | custom-call | tf_op jit(solution)/shard_map/stack/pallas_call | solution.py:528
  286.5 0.0 copy-start.2
  286.5 3.9 %copy.13 = bf16[1,2048,768]{2,1,0:T(8,128)(2,1)} copy(bf16[1,2048,768]{2,1,0:T(8,128)(2,1)} %get-tuple-element.16) | data formatting | bytes 6291456
  290.4 0.0 copy-done.2
  290.4 0.0 copy-start.1
  290.4 1.0 copy.14
  291.4 0.7 copy-done.1
  292.1 0.0 copy-start
  292.1 1.0 copy.15
  293.1 0.7 copy-done
  293.7 1.0 copy.16
Async XLA Ops:
  286.5 3.9 %copy-start.2 = (bf16[2,96,3072]{2,1,0:T(8,128)(2,1)S(1)}, bf16[2,96,3072]{2,1,0:T(8,128)(2,1)}, u32[]{:S(2)}) copy-start(bf16[2,96,3072]{2,1,0:T(8,128)(2,1)} %get-tuple-element.17) | copy-start | bytes 3538948
  290.4 1.7 copy-start.1
  292.1 1.7 copy-start

commit v3 on v2

--- a/solution.py
+++ b/solution.py
@@ -12,6 +12,7 @@
 LANES = 128
 NT = (((1,), (1,)), ((), ()))
 G, U, D = range(3)
+PIECES = (8, 1, 1, 1)
 
 
 def dot(a, b, dims=(((1,), (0,)), ((), ()))):
@@ -27,12 +28,12 @@
 
 
 def kernel(size, x_hbm, dy_hbm, wg_hbm, wu_hbm, wd_hbm,
-           dx_hbm, og_hbm, ou_hbm, od_hbm, fg, fu, fd,
+           dx_hbm, og_hbm, ou_hbm, od_hbm, fg, fu, fd, kept,
            own_g, own_u, own_d, sgu, sd, h, a, at, dout, dt, da, act, dgu,
            pg, pu, pd, sib_g, sib_u, sib_d, send_a_g, send_a_d, send_b_g, send_b_d,
            ra_g, ra_d, rb_g, rb_d, out_g, out_d,
            ag_send, ag_recv, own_sem, own_out, slot_sem, in_sem,
-           sib_send, sib_recv, a_send, a_recv, b_send, b_recv, out_sem, credit):
+           sib_send, sib_recv, a_send, a_recv, b_send, b_recv, out_sem, keep_sem, credit):
     layers, chunks, rows, d, ff_chunk, tokens = (
         size[k] for k in ("layers", "chunks", "rows", "d", "ff_chunk", "tokens"))
     n = size["n"]
@@ -255,6 +256,12 @@
         back = (g * s - wide * (s * s * s * along * (1.0 / d))).astype(BF16)
         dout[r, :] = (dout[r, :].astype(F32) + back.astype(F32)).astype(BF16)
 
+    keep = pltpu.make_async_copy(dgu, kept, keep_sem.at[tokens // TI])
+
+    def again(i):
+        r = pl.ds(i * TI, TI)
+        return pltpu.make_async_copy(kept.at[r], dgu.at[r], keep_sem.at[i])
+
     part, sib = (pg, pu, pd), (sib_g, sib_u, sib_d)
     view = lambda pair, m: pair[0].at[m] if m != D else pair[1]
     sa = [view((send_a_g, send_a_d), m) for m in range(3)]
@@ -313,6 +320,11 @@
         for i in range(2):
             rs_b(m, i).start()
 
+    def reduce_part(s, j):
+        if j == 0:
+            rs2(s, D)
+        rs3(j)
+
     def out_copies(s, m):
         l, k = layers - 1 - s // chunks, lax.rem(s, chunks)
         if m == D:
@@ -409,26 +421,40 @@
         for m in range(3):
             fetch(0, s, m).wait()
 
+        @pl.when(k == units - 1)
+        def _():
+            keep.wait()
+
         def strip(b):
             for j in range(8):
                 @pl.when(jnp.logical_and(more, b == j * strips // 8))
                 def _():
                     gather_part(q_next, j)
 
+            for j in range(3):
+                @pl.when(jnp.logical_and(k == units - 1, b == j))
+                def _():
+                    reduce_part(k - 1, j)
+
             for i in range(tokens // TH):
                 hidden_tile(s, i, b)
 
         loop(strips, strip)
 
-        @pl.when(k > 0)
-        def _():
-            for m in range(3):
+        @pl.when(k == units - 2)
+        def _():
+            keep.start()
+
+        def done(m):
+            @pl.when(k > 0)
+            def _():
                 rs4(k - 1, m)
 
         @pl.when(jnp.logical_and(lax.rem(k, chunks) == chunks - 1, k < units - 1))
         def _():
             load_x(a).start()
 
+        done(G)
         loop(blocks, lambda b: weights_up(b, dg, pg))
         rs1(k, G)
 
@@ -437,10 +463,12 @@
             g1(last, U)
             g1(last, D)
 
+        done(U)
         loop(blocks, lambda b: weights_up(b, du, pu))
         rs1(k, U)
         rs2(k, G)
 
+        done(D)
         loop(blocks, weights_down)
         rs1(k, D)
         rs2(k, U)
@@ -454,20 +482,30 @@
             for m in range(3):
                 fetch(q_next, 1 - s, m).start()
 
-        def back(i):
-            @pl.when(i == 1)
-            def _():
-                rs2(k, D)
-                rs3(G)
-
-            @pl.when(i == 2)
-            def _():
-                rs3(U)
-
-            input_tile(s, i, first)
-
-        loop(tokens // TI, back)
-        rs3(D)
+        @pl.when(k != units - 2)
+        def _():
+            def back(i):
+                for j in range(2):
+                    @pl.when(i == j + 1)
+                    def _():
+                        reduce_part(k, j)
+
+                input_tile(s, i, first)
+
+                @pl.when(k == units - 1)
+                def _():
+                    again(i).start()
+
+            loop(tokens // TI, back)
+            reduce_part(k, 2)
+
+        @pl.when(k == units - 1)
+        def _():
+            def rest(i):
+                again(i).wait()
+                input_tile(1 - s, i, False)
+
+            loop(tokens // TI, rest)
 
         @pl.when(lax.rem(k, chunks) == chunks - 1)
         def _():
@@ -491,6 +529,37 @@
             g_end(q, m)
 
     loop(units, ends)
+
+
+def finish(arrays):
+    def copy_all(*refs):
+        k = len(arrays)
+        ins, outs, held, (sem_in, sem_out) = refs[:k], refs[k:2 * k], refs[2 * k:3 * k], refs[3 * k:]
+        pieces = []
+        for j in range(k):
+            rows = arrays[j].shape[1] // PIECES[j]
+            pieces += [(j, l, pl.ds(p * rows, rows)) for l in range(arrays[j].shape[0]) for p in range(PIECES[j])]
+        into = [pltpu.make_async_copy(ins[j].at[l, r], held[j].at[l, r], sem_in.at[i]) for i, (j, l, r) in enumerate(pieces)]
+        back = [pltpu.make_async_copy(held[j].at[l, r], outs[j].at[l, r], sem_out.at[i]) for i, (j, l, r) in enumerate(pieces)]
+        for cp in into:
+            cp.start()
+        for a, b in zip(into, back):
+            a.wait()
+            b.start()
+        for b in back:
+            b.wait()
+
+    hbm = pl.BlockSpec(memory_space=pl.ANY)
+    count = sum(a.shape[0] * p for a, p in zip(arrays, PIECES))
+    return tuple(pl.pallas_call(
+        copy_all,
+        out_shape=[jax.ShapeDtypeStruct(a.shape, a.dtype) for a in arrays],
+        in_specs=[hbm] * len(arrays),
+        out_specs=[hbm] * len(arrays),
+        scratch_shapes=[pltpu.VMEM(a.shape, a.dtype) for a in arrays] + [pltpu.SemaphoreType.DMA((count,))] * 2,
+        compiler_params=pltpu.CompilerParams(vmem_limit_bytes=67_043_328),
+        name="finish",
+    )(*arrays))
 
 
 def solution(mesh):
@@ -522,7 +591,7 @@
             vm((2, 2, rows // 2, ff_chunk), BF16), vm((2, LANES // 2, d), BF16), vm((2, 2, *up), BF16), vm((2, *down), BF16),
             vm((2, *up), BF16), vm(down, BF16),
             dma((units, 3, 14)), dma((units, 3, 14)), dma((3, units, n)), dma((3, units)), dma((2, 3)), dma((2,)),
-            dma((3,)), dma((3,)), dma((3, 2)), dma((3, 2)), dma((3, 2)), dma((3, 2)), dma((3, n)),
+            dma((3,)), dma((3,)), dma((3, 2)), dma((3, 2)), dma((3, 2)), dma((3, 2)), dma((3, n)), dma((tokens // 512 + 1,)),
             pltpu.SemaphoreType.REGULAR((3,)),
         ]
         outs = pl.pallas_call(
@@ -530,15 +599,16 @@
             out_shape=[
                 sds(x.shape, BF16), sds(wg.shape, BF16), sds(wu.shape, BF16), sds(wd.shape, BF16),
                 sds((units, d, ff_chunk), BF16), sds((units, d, ff_chunk), BF16), sds((units, ff_chunk, d), BF16),
+                sds((tokens, 2 * ff_chunk), BF16),
             ],
             in_specs=[hbm] * 5,
-            out_specs=[hbm] * 7,
+            out_specs=[hbm] * 8,
             scratch_shapes=scratch,
             compiler_params=pltpu.CompilerParams(
                 collective_id=0, has_side_effects=True, vmem_limit_bytes=67_043_328),
             name="stack",
         )(x, dy, wg, wu, wd)
-        return tuple(outs[:4])
+        return finish(outs[:4])
 
     seq, w = P(("rep", "dp"), None, None), P(None, "dp", None)
     return jax.shard_map(step, mesh=mesh, in_specs=(seq, seq, w, w, w),

time: 295 us -> 288 us (0.976)
  local copies, waits for them, and re-layouts: 8.26 us -> 0 us
    unnamed x10 -> x0, local copies, waits for them, and re-layouts: 8.26 us -> none
    pallas_call x0 -> x1, Pallas kernels: none -> 5.52 us  [finish(): pl.pallas_call(copy_all, out_shape=[jax.ShapeDtypeStruct(a.shape, a.dtype...]
    pallas_call x1, Pallas kernels: 286 us -> 281 us  [step(): pl.pallas_call(functools.partial(kernel, size), out_shape=[sds(x.shape, B...]
where the time goes in v3:
time: 288 us
  Pallas kernels  287 us (100%)
    pallas_call x1, Pallas kernels, step(): pl.pallas_call(functools.partial(kernel, size), out_shape=[sds(x.shape, B...  281 us

profile of v3, /device:TPU:112, one launch (start us, length us, event | category | flops | bytes accessed | tf_op | source)
XLA Modules:
  0.0 287.5 jit_solution(2636482873710948387)
XLA Ops:
  0.6 281.2 %stack.1 = (bf16[1,2048,768]{2,1,0:T(8,128)(2,1)}, bf16[2,96,3072]{2,1,0:T(8,128)(2,1)}, bf16[2,96,3072]{2,1,0:T(8,128)(2,1)}, bf16[2,384,768]{2,1,0:T(8,128)(2,...) custom-call(bf16[1,2048,768]{2,1,0:T(8,128)(2,1)} %x_hbm.1, ...), custom_call_target="tpu_custom_call" | custom-call | tf_op jit(solution)/shard_map/stack/pallas_call | solution.py:597
  281.8 5.5 %finish.1 = (bf16[1,2048,768]{2,1,0:T(8,128)(2,1)}, bf16[2,96,3072]{2,1,0:T(8,128)(2,1)}, bf16[2,96,3072]{2,1,0:T(8,128)(2,1)}, bf16[2,384,768]{2,1,0:T(8,128)(2,1)}) custom-call(bf16[1,2048,768]{2,1,0:T(8,128)(2,1)} %get-tuple-element.8.refs_0_, bf16[2,96,3072]{2,1,0:T(8,128)(2,1)} %get-tuple-element.9.refs_1_, ...), custom_call_target="tpu_custom_call" | custom-call | tf_op jit(solution)/shard_map/finish/pallas_call | solution.py:554

commit v4 on v3

--- a/solution.py
+++ b/solution.py
@@ -178,23 +178,14 @@
     def scale_of(wide):
         return lax.rsqrt(jnp.mean(wide * wide, -1, keepdims=True) + 1e-6)
 
-    def norm_tile(i, src=h):
-        r = pl.ds(i * TP, TP)
-        wide = src[r, :].astype(F32)
+    def normed(wide, r):
         a_tile = (wide * scale_of(wide)).astype(BF16)
         a[r, :] = a_tile
         return a_tile
 
-    def transpose_a(i):
-        cols = pl.ds(pl.multiple_of(i * TP, TP), TP)
-        at[:, cols] = norm_tile(i).T
-
-    def restart(i):
+    def norm_tile(i):
         r = pl.ds(i * TP, TP)
-        cols = pl.ds(pl.multiple_of(i * TP, TP), TP)
-        h[r, :] = a[r, :]
-        at[:, cols] = norm_tile(i, a).T
-        dt[:, cols] = dout[r, :].T
+        normed(h[r, :].astype(F32), r)
 
     def transpose_dout(i):
         cols = pl.ds(pl.multiple_of(i * TP, TP), TP)
@@ -254,7 +245,17 @@
         g = da[r, :].astype(BF16).astype(F32)
         along = jnp.sum(g * wide, -1, keepdims=True)
         back = (g * s - wide * (s * s * s * along * (1.0 / d))).astype(BF16)
-        dout[r, :] = (dout[r, :].astype(F32) + back.astype(F32)).astype(BF16)
+        by_input = (dout[r, :].astype(F32) + back.astype(F32)).astype(BF16)
+        dout[r, :] = by_input
+        return by_input
+
+    def next_layer(i):
+        r = pl.ds(i * TP, TP)
+        cols = pl.ds(pl.multiple_of(i * TP, TP), TP)
+        dt[:, cols] = norm_back(i).T
+        came = a[r, :]
+        h[r, :] = came
+        at[:, cols] = normed(came.astype(F32), r).T
 
     keep = pltpu.make_async_copy(dgu, kept, keep_sem.at[tokens // TI])
 
@@ -380,8 +381,17 @@
         gather_part(0, i)
     gather_end(0, 0)
 
+    def ends(q):
+        for m in range(3):
+            g_end(q, m)
+
     def forward(k, carry):
         s = lax.rem(k, 2)
+
+        @pl.when(k > 0)
+        def _():
+            ends(k - 1)
+
         for m in range(3):
             fetch(k, s, m).wait()
 
@@ -402,10 +412,12 @@
 
     def add_hidden(i):
         r = pl.ds(i * TP, TP)
-        h[r, :] = (h[r, :].astype(F32) + da[r, :].astype(BF16).astype(F32)).astype(BF16)
+        cols = pl.ds(pl.multiple_of(i * TP, TP), TP)
+        after = (h[r, :].astype(F32) + da[r, :].astype(BF16).astype(F32)).astype(BF16)
+        h[r, :] = after
+        at[:, cols] = normed(after.astype(F32), r).T
 
     loop(prep_tiles, add_hidden)
-    loop(prep_tiles, transpose_a)
 
     def backward(k, carry):
         s = lax.rem(k + fwd, 2)
@@ -413,33 +425,41 @@
         more = k < units - fwd - 1
         first = lax.rem(k, chunks) == 0
 
-        @pl.when(jnp.logical_and(first, k > 0))
-        def _():
-            load_x(a).wait()
-            loop(prep_tiles, restart)
-
         for m in range(3):
             fetch(0, s, m).wait()
 
+        @pl.when(jnp.logical_and(k < units - 1, jnp.logical_not(more)))
+        def _():
+            for m in range(3):
+                fetch(q_next, 1 - s, m).start()
+
         @pl.when(k == units - 1)
         def _():
             keep.wait()
 
         def strip(b):
-            for j in range(8):
-                @pl.when(jnp.logical_and(more, b == j * strips // 8))
+            for j, parts in enumerate(((0, 1), (2, 3, 4))):
+                @pl.when(jnp.logical_and(more, b == j))
                 def _():
-                    gather_part(q_next, j)
-
-            for j in range(3):
+                    for i in parts:
+                        gather_part(q_next, i)
+
+            for j, parts in enumerate(((0,), (1, 2))):
                 @pl.when(jnp.logical_and(k == units - 1, b == j))
                 def _():
-                    reduce_part(k - 1, j)
-
-            for i in range(tokens // TH):
-                hidden_tile(s, i, b)
-
-        loop(strips, strip)
+                    for i in parts:
+                        reduce_part(k - 1, i)
+
+            for t in range(strips // 2):
+                for i in range(tokens // TH):
+                    hidden_tile(s, i, b * (strips // 2) + t)
+
+        loop(2, strip)
+
+        @pl.when(more)
+        def _():
+            for i in (5, 6, 7):
+                gather_part(q_next, i)
 
         @pl.when(k == units - 2)
         def _():
@@ -477,16 +497,11 @@
         def _():
             gather_end(q_next, 1 - s)
 
-        @pl.when(jnp.logical_and(k < units - 1, jnp.logical_not(more)))
-        def _():
-            for m in range(3):
-                fetch(q_next, 1 - s, m).start()
-
         @pl.when(k != units - 2)
         def _():
             def back(i):
                 for j in range(2):
-                    @pl.when(i == j + 1)
+                    @pl.when(i == 1 + 2 * j)
                     def _():
                         reduce_part(k, j)
 
@@ -509,7 +524,14 @@
 
         @pl.when(lax.rem(k, chunks) == chunks - 1)
         def _():
-            loop(prep_tiles, norm_back)
+            @pl.when(k < units - 1)
+            def _():
+                load_x(a).wait()
+                loop(prep_tiles, next_layer)
+
+            @pl.when(k == units - 1)
+            def _():
+                loop(prep_tiles, norm_back)
 
 
         return carry
@@ -517,18 +539,13 @@
     lax.fori_loop(0, units, backward, 0)
     store_dx = pltpu.make_async_copy(dout, dx_hbm.at[0], in_sem.at[1])
     store_dx.start()
+    loop(units - fwd + 1, lambda q: ends(q + fwd - 1))
     for m in range(3):
         rs4(units - 1, m)
     for m in range(3):
         for cp in out_copies(units - 1, m):
             cp.wait()
     store_dx.wait()
-
-    def ends(q):
-        for m in range(3):
-            g_end(q, m)
-
-    loop(units, ends)
 
 
 def finish(arrays):

time: 288 us -> 282 us (0.979)
  Pallas kernels: 287 us -> 281 us
    pallas_call x1, Pallas kernels: 281 us -> 275 us  [step(): pl.pallas_call(functools.partial(kernel, size), out_shape=[sds(x.shape, B...]
where the time goes in v4:
time: 282 us; the launch traced here: 281 us
  Pallas kernels  281 us (100%)
    pallas_call x1, Pallas kernels, step(): pl.pallas_call(functools.partial(kernel, size), out_shape=[sds(x.shape, B...  275 us

profile of v4, /device:TPU:112, one launch (start us, length us, event | category | flops | bytes accessed | tf_op | source)
XLA Modules:
  0.0 281.3 jit_solution(257807957153167334)
XLA Ops:
  0.6 275.0 %stack.1 = (bf16[1,2048,768]{2,1,0:T(8,128)(2,1)}, bf16[2,96,3072]{2,1,0:T(8,128)(2,1)}, bf16[2,96,3072]{2,1,0:T(8,128)(2,1)}, bf16[2,384,768]{2,1,0:T(8,128)(2,...) custom-call(bf16[1,2048,768]{2,1,0:T(8,128)(2,1)} %x_hbm.1, ...), custom_call_target="tpu_custom_call" | custom-call | tf_op jit(solution)/shard_map/stack/pallas_call | solution.py:614
  275.6 5.5 %finish.1 = (bf16[1,2048,768]{2,1,0:T(8,128)(2,1)}, bf16[2,96,3072]{2,1,0:T(8,128)(2,1)}, bf16[2,96,3072]{2,1,0:T(8,128)(2,1)}, bf16[2,384,768]{2,1,0:T(8,128)(2,1)}) custom-call(bf16[1,2048,768]{2,1,0:T(8,128)(2,1)} %get-tuple-element.8.refs_0_, bf16[2,96,3072]{2,1,0:T(8,128)(2,1)} %get-tuple-element.9.refs_1_, ...), custom_call_target="tpu_custom_call" | custom-call | tf_op jit(solution)/shard_map/finish/pallas_call | solution.py:571
